TPU v7x, 32 devices: a whole 2x2x4 slice. The times are simulated.
32 devices in a mesh: sub: 8 (over z, y), grp: 4 (over x, core).
Axes of the slice: x: 2, y: 2, z: 4, core: 2. Of those that a mesh axis runs over, the one named last changes fastest.
Arguments:
- rr_inverse: float32 [64, 512, 512], P(('sub', 'grp')), may hold values from -4 to 4, as said below
- corner_modes: float32 [64, 64, 512], P(('sub', 'grp')), may hold values from -0.5 to 0.5
- coarse_inverse: float32 [2048, 2048], P(('sub', 'grp')), may hold values from -1 to 1, as said below
- inertia: float32 [64, 512], P(('sub', 'grp')), may hold values from 0.5 to 2
- disp_now: float32 [8, 64, 512], P(None, ('sub', 'grp')), may hold values from -4 to 4
- vel_now: float32 [8, 64, 512], P(None, ('sub', 'grp')), may hold values from -4 to 4
- acc_now: float32 [8, 64, 512], P(None, ('sub', 'grp')), may hold values from -8 to 8
- load_next: float32 [8, 64, 512], P(None, ('sub', 'grp')), may hold values from -10 to 10
- basis_rows: float32 [32768, 256], P(('sub', 'grp')), may hold values from -0.03125 to 0.03125
- piece_owner: int32 [32], replicated, may hold values from 0 to 31, each once
Outputs:
- disp_new: float32 [8, 64, 512], P(None, ('sub', 'grp'))
- vel_new: float32 [8, 64, 512], P(None, ('sub', 'grp'))
- projection: float32 [256, 8], replicated
- r_factor: float32 [8, 8], replicated
- new_columns: float32 [8, 32768], P(None, ('sub', 'grp'))
Inputs may be any that keep to these rules, and one draw needn't show every extreme that they name: piece_owner is a permutation. `rr_inverse`: each of the 64 blocks is symmetric positive definite. `coarse_inverse`: symmetric positive definite.
All inputs are finite; a program needn't handle non-finite values.
Results may differ from a plain program's by a relative error of at most 0.00018.
Values sent between devices are 32-bit elements; how exact they have to be, the bound alone decides.
A program may use at most 64 MiB of HBM per device.

v0:
```python
import math
import jax
import jax.numpy as jnp
from jax import lax
from jax.sharding import PartitionSpec as P

NC = 32
ITERS = 2
NI = 128
highest = lax.Precision.HIGHEST
time_step = 0.5
newmark_beta = 0.25
newmark_gamma = 0.5


def shifted(array, axis, by):
    count = lax.axis_size(axis)
    return lax.ppermute(array, axis, [(i, (i + by) % count) for i in range(count)])


def contract(segment, matrix_rows):
    return lax.dot_general(segment, matrix_rows, (((1,), (1,)), ((), ())), precision=highest)


def shards(
    rr_inverse,
    corner_modes,
    coarse_inverse,
    inertia,
    disp_now,
    vel_now,
    acc_now,
    load_next,
    basis_rows,
    piece_owner,
):
    case_count, sub_count, unknowns = disp_now.shape
    coarse_total = coarse_inverse.shape[1]
    row_count = sub_count * NC
    shifted_rows = jnp.roll(coarse_inverse, NC, axis=1)
    coarse_pairs = jnp.concatenate(
        [
            shifted_rows.reshape(row_count, coarse_total // NC, NC),
            coarse_inverse.reshape(row_count, coarse_total // NC, NC),
        ],
        axis=2,
    ).reshape(row_count, 2 * coarse_total)

    def apply_green(field):
        local_part = jnp.einsum("jab,cjb->cja", rr_inverse, field, precision=highest)
        corner_terms = jnp.einsum("jmb,cjb->cjm", corner_modes, field, precision=highest)
        flat_terms = corner_terms.reshape(case_count, sub_count * 2 * NC)
        owned_sums = contract(
            lax.all_gather(flat_terms, ("sub", "grp"), axis=1, tiled=True), coarse_pairs
        )
        previous = shifted(owned_sums[:, row_count - NC :], ("sub", "grp"), 1)
        owned_blocks = owned_sums.reshape(case_count, sub_count, NC)
        left_values = jnp.concatenate(
            [previous.reshape(case_count, 1, NC), owned_blocks[:, :-1]], axis=1
        )
        coarse_values = jnp.concatenate([left_values, owned_blocks], axis=2)
        return local_part + jnp.einsum(
            "jmb,cjm->cjb", corner_modes, coarse_values, precision=highest
        )

    def interface_jump(field):
        following = shifted(field[:, :1, :NI], ("sub", "grp"), -1)
        first_parts = jnp.concatenate([field[:, 1:, :NI], following], axis=1)
        return field[:, :, unknowns - NI :] - first_parts

    def squared_norm(values):
        return lax.psum(jnp.sum(values * values, axis=(1, 2)), ("sub", "grp"))

    right_side = load_next + inertia[None] * (
        disp_now + time_step * vel_now + (0.5 - newmark_beta) * time_step * time_step * acc_now
    )
    green_rhs = apply_green(right_side)
    residual = interface_jump(green_rhs)
    carried = green_rhs
    direction = residual
    norm_now = squared_norm(residual)
    for iteration in range(ITERS):
        earlier = shifted(direction[:, -1:], ("sub", "grp"), 1)
        left_parts = jnp.concatenate([earlier, direction[:, :-1]], axis=1)
        middle = jnp.zeros((case_count, sub_count, unknowns - 2 * NI), jnp.float32)
        image_field = apply_green(jnp.concatenate([-left_parts, middle, direction], axis=2))
        image = interface_jump(image_field)
        curvature = lax.psum(jnp.sum(direction * image, axis=(1, 2)), ("sub", "grp"))
        alpha = (norm_now / curvature)[:, None, None]
        carried = carried - alpha * image_field
        residual = residual - alpha * image
        if iteration + 1 < ITERS:
            norm_next = squared_norm(residual)
            direction = residual + (norm_next / norm_now)[:, None, None] * direction
            norm_now = norm_next
    accel_new = (
        (carried - disp_now) / (newmark_beta * time_step * time_step)
        - vel_now / (newmark_beta * time_step)
        - (0.5 / newmark_beta - 1.0) * acc_now
    )
    vel_new = vel_now + time_step * ((1.0 - newmark_gamma) * acc_now + newmark_gamma * accel_new)
    piece_total = lax.axis_size(("sub", "grp"))
    piece_rows = unknowns // piece_total
    inverse = (
        jnp.zeros((piece_total,), jnp.int32)
        .at[piece_owner]
        .set(jnp.arange(piece_total, dtype=jnp.int32))
    )
    outgoing = carried.reshape(case_count, sub_count, piece_total, piece_rows)[:, :, inverse, :]
    outgoing = jnp.transpose(outgoing, (0, 2, 1, 3)).reshape(
        case_count, piece_total * sub_count * piece_rows
    )
    received = lax.all_to_all(outgoing, ("sub", "grp"), split_axis=1, concat_axis=1, tiled=True)
    projection_part = lax.dot_general(
        basis_rows, received, (((0,), (1,)), ((), ())), precision=highest
    )
    projection = lax.psum(projection_part, ("sub", "grp"))
    remainder = received - lax.dot_general(
        projection, basis_rows, (((0,), (1,)), ((), ())), precision=highest
    )
    gram_local = lax.dot_general(remainder, remainder, (((1,), (1,)), ((), ())), precision=highest)
    lower = jnp.linalg.cholesky(lax.psum(gram_local, ("sub", "grp")))
    scale_rows = math.sqrt(received.shape[1] * piece_total)
    new_columns = jax.scipy.linalg.solve_triangular(lower, remainder, lower=True) * scale_rows
    r_factor = lower.T / scale_rows
    return (carried, vel_new, projection, r_factor, new_columns)


def solution(mesh):
    return jax.shard_map(
        shards,
        mesh=mesh,
        in_specs=(
            P(("sub", "grp"), None, None),
            P(("sub", "grp"), None, None),
            P(("sub", "grp"), None),
            P(("sub", "grp"), None),
            P(None, ("sub", "grp"), None),
            P(None, ("sub", "grp"), None),
            P(None, ("sub", "grp"), None),
            P(None, ("sub", "grp"), None),
            P(("sub", "grp"), None),
            P(),
        ),
        out_specs=(
            P(None, ("sub", "grp"), None),
            P(None, ("sub", "grp"), None),
            P(),
            P(),
            P(None, ("sub", "grp")),
        ),
        check_vma=False,
    )
```

profile of v0, /device:TPU:0, one launch (start us, length us, event | category | flops | bytes accessed | tf_op | source)
XLA Modules:
  0.0 396.2 jit_solution(17063526511338648422)
XLA Ops:
  0.7 1.5 copy.65
  2.2 1.1 slice.101
  3.4 0.3 convolution_bitcast_fusion.3
  3.8 43.6 %all_gather.9 = f32[8,4096]{1,0:T(8,128)S(1)} all-gather(f32[8,128]{1,0:T(8,128)S(1)} %reshape.67), channel_id=1, replica_groups=mesh['sub'=8,'grp'=4] {'sub','grp'}, dimensions={1}, use_global_device_ids=true | all-gather | bytes 135168 | tf_op jit(solution)/shard_map/all_gather | solution.py:54
  47.4 1.3 pad_maximum_fusion.1
  48.7 0.2 pad_maximum_fusion
  48.9 1.3 copy-done.1
  50.2 1.1 fusion.49
  51.4 0.4 collective-permute-start
  51.8 1.8 fusion.10
  53.7 4.4 %collective-permute-done = f32[8,32]{1,0:T(8,128)S(1)} collective-permute-done((f32[8,32]{1,0:T(8,128)S(1)}, f32[8,32]{1,0:T(8,128)S(1)}, u32[]{:S(2)}, u32[]{:S(2)}) %collective-permute-start) | collective-permute-done | bytes 1056 | tf_op jit(solution)/shard_map/ppermute | solution.py:18
  58.1 0.3 fusion.2
  58.4 0.7 collective-permute-start.1
  59.0 1.3 collective-permute-done.1
  60.4 6.6 %collective-permute-done.2 = f32[8,1,128]{2,0,1:T(8,128)S(1)} collective-permute-done((f32[8,1,128]{2,0,1:T(8,128)S(1)}, f32[8,1,128]{2,0,1:T(8,128)S(1)}, u32[]{:S(2)}, u32[]{:S(2)}) %collective-permute-start.2) | collective-permute-done | bytes 4128 | tf_op jit(solution)/shard_map/ppermute | solution.py:18
  67.0 0.3 convolution_bitcast_fusion.2
  67.4 36.7 %all_gather.10 = f32[8,4096]{1,0:T(8,128)S(1)} all-gather(f32[8,128]{1,0:T(8,128)S(1)} %reshape.73), channel_id=1, replica_groups=mesh['sub'=8,'grp'=4] {'sub','grp'}, dimensions={1}, use_global_device_ids=true | all-gather | bytes 135168 | tf_op jit(solution)/shard_map/all_gather | solution.py:54
  104.1 2.7 fusion.50
  106.9 0.4 collective-permute-start.3
  107.2 1.8 fusion.5
  109.1 4.4 %collective-permute-done.3 = f32[8,32]{1,0:T(8,128)S(1)} collective-permute-done((f32[8,32]{1,0:T(8,128)S(1)}, f32[8,32]{1,0:T(8,128)S(1)}, u32[]{:S(2)}, u32[]{:S(2)}) %collective-permute-start.3) | collective-permute-done | bytes 1056 | tf_op jit(solution)/shard_map/ppermute | solution.py:18
  113.5 0.3 fusion.1
  113.8 0.7 collective-permute-start.4
  114.5 1.3 collective-permute-done.4
  115.8 0.1 multiply_reduce_fusion.1
  116.0 38.1 %all-reduce = (f32[8]{0:T(128)S(1)}, f32[8]{0:T(128)S(1)}) all-reduce(f32[8]{0:T(128)S(1)} %get-tuple-element.21, f32[8]{0:T(128)S(1)} %get-tuple-element.20), channel_id=1, replica_groups=mesh['sub'=8,'grp'=4] {'sub','grp'}, use_global_device_ids=true, to_apply=%region_1.2 | all-reduce | flops 16 | bytes 128 | tf_op jit(solution)/shard_map/psum | solution.py:72
  154.1 0.2 multiply_reduce_fusion
  154.3 42.1 %psum.44 = f32[8]{0:T(128)S(1)} all-reduce(f32[8]{0:T(128)S(1)} %multiply_reduce_fusion), channel_id=1, replica_groups=mesh['sub'=8,'grp'=4] {'sub','grp'}, use_global_device_ids=true, to_apply=%region_5.6 | all-reduce | flops 8 | bytes 64 | tf_op jit(solution)/shard_map/psum | solution.py:72
  196.5 0.7 scatter_custom_fusion
  197.2 5.9 %collective-permute-done.5 = f32[8,1,128]{2,0,1:T(8,128)S(1)} collective-permute-done((f32[8,1,128]{2,0,1:T(8,128)S(1)}, f32[8,1,128]{2,0,1:T(8,128)S(1)}, u32[]{:S(2)}, u32[]{:S(2)}) %collective-permute-start.5) | collective-permute-done | bytes 4128 | tf_op jit(solution)/shard_map/ppermute | solution.py:18
  203.1 0.3 convolution_bitcast_fusion.1
  203.5 36.7 %all_gather.11 = f32[8,4096]{1,0:T(8,128)S(1)} all-gather(f32[8,128]{1,0:T(8,128)S(1)} %reshape.76), channel_id=1, replica_groups=mesh['sub'=8,'grp'=4] {'sub','grp'}, dimensions={1}, use_global_device_ids=true | all-gather | bytes 135168 | tf_op jit(solution)/shard_map/all_gather | solution.py:54
  240.2 2.7 fusion.51
  242.9 0.5 collective-permute-start.6
  243.4 2.5 fusion.6
  246.0 3.7 collective-permute-done.6
  249.7 1.0 fusion
  250.8 1.4 collective-permute-start.7
  252.2 1.3 collective-permute-done.7
  253.5 0.1 fusion.17
  253.6 38.1 %psum.45 = f32[8]{0:T(128)S(1)} all-reduce(f32[8]{0:T(128)S(1)} %fusion.17), channel_id=1, replica_groups=mesh['sub'=8,'grp'=4] {'sub','grp'}, use_global_device_ids=true, to_apply=%region_7.8 | all-reduce | flops 8 | bytes 64 | tf_op jit(solution)/shard_map/psum | solution.py:88
  291.7 1.5 fusion.4
  293.2 0.1 reshape.79
  293.3 0.8 copy.81
  294.2 1.5 gather_fusion
  295.7 0.2 copy.82
  296.0 0.7 reshape.100
  296.7 6.5 %all-to-all-start = ((f32[32,1,256]{2,1,0:T(1,128)}), f32[32,1,256]{2,1,0:T(1,128)S(1)}, u32[]{:S(2)}, u32[]{:S(2)}) async-start(f32[32,1,256]{2,1,0:T(1,128)} %reshape.100), calls=%async_computation | async-start | bytes 65536 | tf_op jit(solution)/shard_map/all_to_all | solution.py:113
  303.2 1.4 copy.88
  304.6 1.4 copy.89
  306.0 4.5 %all-to-all-done = f32[32,1,256]{2,1,0:T(1,128)S(1)} async-done(((f32[32,1,256]{2,1,0:T(1,128)}), f32[32,1,256]{2,1,0:T(1,128)S(1)}, u32[]{:S(2)}, u32[]{:S(2)}) %all-to-all-start) | async-done | bytes 32800 | tf_op jit(solution)/shard_map/all_to_all | solution.py:113
  310.5 0.5 broadcast.116
  311.0 0.7 reduce.6
  311.9 0.5 convolution_bitcast_fusion
  312.5 38.3 %psum.46 = f32[256,8]{0,1:T(8,128)S(1)} all-reduce(f32[256,8]{0,1:T(8,128)S(1)} %convolution_bitcast_fusion), channel_id=1, replica_groups=mesh['sub'=8,'grp'=4] {'sub','grp'}, use_global_device_ids=true, to_apply=%region_9.10 | all-reduce | flops 2048 | bytes 16384 | tf_op jit(solution)/shard_map/psum | solution.py:117
  350.7 1.0 convolution_subtract_fusion
  351.7 0.2 fusion.52
  351.8 40.1 %psum.47 = f32[8,8]{0,1:T(8,128)S(1)} all-reduce(f32[8,8]{0,1:T(8,128)S(1)} %fusion.52), channel_id=1, replica_groups=mesh['sub'=8,'grp'=4] {'sub','grp'}, use_global_device_ids=true, to_apply=%region_10.11 | all-reduce | flops 64 | bytes 512 | tf_op jit(solution)/shard_map/psum | solution.py:122
  392.0 0.7 cholesky.18
  392.7 0.6 compare_reduce_fusion
  393.4 0.6 select_bitcast_fusion
  394.0 0.6 custom-call.7
  394.7 0.9 convolution_multiply_fusion
  395.5 0.7 copy.90
  (70 shorter events, 1.5 us)
Async XLA Ops:
  0.6 51.1 %copy-start = (f32[2,512,512]{2,1,0:T(8,128)S(1)}, f32[2,512,512]{2,1,0:T(8,128)}, u32[]{:S(2)}) copy-start(f32[2,512,512]{2,1,0:T(8,128)} %param.10) | copy-start | bytes 6291460
  0.6 2.7 copy-start.6
  0.7 2.7 copy-start.7
  0.7 2.6 copy-start.5
  0.7 2.7 copy-start.2
  2.2 1.1 copy-start.9
  2.2 1.1 copy-start.10
  48.9 1.4 copy-start.1
  51.4 6.7 %collective-permute-start = (f32[8,32]{1,0:T(8,128)S(1)}, f32[8,32]{1,0:T(8,128)S(1)}, u32[]{:S(2)}, u32[]{:S(2)}) collective-permute-start(f32[8,32]{1,0:T(8,128)S(1)} %slice.79), channel_id=1, source_target_pairs={{0,1},{1,2},{2,3},{3,4},{4,5},{5,6},{6,7},{7,8},{8,9},{9,10},{10,1... | collective-permute-start | bytes 3080 | tf_op jit(solution)/shard_map/ppermute | solution.py:18
  58.4 2.0 collective-permute-start.1
  60.4 6.6 %collective-permute-start.2 = (f32[8,1,128]{2,0,1:T(8,128)S(1)}, f32[8,1,128]{2,0,1:T(8,128)S(1)}, u32[]{:S(2)}, u32[]{:S(2)}) collective-permute-start(f32[8,1,128]{2,0,1:T(8,128)S(1)} %get-tuple-element.34), channel_id=1, source_target_pairs={{0,1},{1,2},{2,3},{3,4},{4,5},{5,6},{6,7},{7,8},{8,9},{9,10},{10,1... | collective-permute-start | bytes 12296 | tf_op jit(solution)/shard_map/ppermute | solution.py:18
  104.1 92.4 %copy-start.11 = (s32[32]{0:T(128)S(1)}, s32[32]{0:T(128)}, u32[]{:S(2)}) copy-start(s32[32]{0:T(128)} %param.19) | copy-start | bytes 388
  106.9 6.6 %collective-permute-start.3 = (f32[8,32]{1,0:T(8,128)S(1)}, f32[8,32]{1,0:T(8,128)S(1)}, u32[]{:S(2)}, u32[]{:S(2)}) collective-permute-start(f32[8,32]{1,0:T(8,128)S(1)} %slice.86), channel_id=1, source_target_pairs={{0,1},{1,2},{2,3},{3,4},{4,5},{5,6},{6,7},{7,8},{8,9},{9,10},{10,1... | collective-permute-start | bytes 3080 | tf_op jit(solution)/shard_map/ppermute | solution.py:18
  113.8 2.0 collective-permute-start.4
  196.4 6.6 %collective-permute-start.5 = (f32[8,1,128]{2,0,1:T(8,128)S(1)}, f32[8,1,128]{2,0,1:T(8,128)S(1)}, u32[]{:S(2)}, u32[]{:S(2)}) collective-permute-start(f32[8,1,128]{2,0,1:T(8,128)S(1)} %get-tuple-element.32), channel_id=1, source_target_pairs={{0,1},{1,2},{2,3},{3,4},{4,5},{5,6},{6,7},{7,8},{8,9},{9,10},{10,1... | collective-permute-start | bytes 12296 | tf_op jit(solution)/shard_map/ppermute | solution.py:18
  242.9 6.8 %collective-permute-start.6 = (f32[8,32]{1,0:T(8,128)S(1)}, f32[8,32]{1,0:T(8,128)S(1)}, u32[]{:S(2)}, u32[]{:S(2)}) collective-permute-start(f32[8,32]{1,0:T(8,128)S(1)} %slice.93), channel_id=1, source_target_pairs={{0,1},{1,2},{2,3},{3,4},{4,5},{5,6},{6,7},{7,8},{8,9},{9,10},{10,1... | collective-permute-start | bytes 3080 | tf_op jit(solution)/shard_map/ppermute | solution.py:18
  245.9 66.0 %copy-start.3 = (f32[1024,256]{1,0:T(8,128)S(1)}, f32[1024,256]{1,0:T(8,128)}, u32[]{:S(2)}) copy-start(f32[1024,256]{1,0:T(8,128)} %param.18) | copy-start | bytes 3145732
  250.8 2.7 collective-permute-start.7
  293.2 2.5 copy-start.4
  296.7 13.7 %all-to-all-start = ((f32[32,1,256]{2,1,0:T(1,128)}), f32[32,1,256]{2,1,0:T(1,128)S(1)}, u32[]{:S(2)}, u32[]{:S(2)}) async-start(f32[32,1,256]{2,1,0:T(1,128)} %reshape.100), calls=%async_computation | async-start | bytes 65536 | tf_op jit(solution)/shard_map/all_to_all | solution.py:113
  350.7 45.5 %copy-start.8 = (f32[256,8]{0,1:T(8,128)}, f32[256,8]{0,1:T(8,128)S(1)}, u32[]{:S(2)}) copy-start(f32[256,8]{0,1:T(8,128)S(1)} %psum.46) | copy-start | bytes 24580
where the time goes:
time: 397 us; the launch traced here: 396 us
  blocking collectives  314 us (79%)
  waiting for transfers between devices  33.4 us (8%)
  matrix products  17.6 us (4%)
  local copies, waits for them, and re-layouts  13.2 us (3%)
  starting transfers between devices  10.5 us (3%)
  other arithmetic  6.97 us (2%)
    all_gather x3, blocking collectives, apply_green(): lax.all_gather(flat_terms, ('sub', 'grp'), axis=1, tiled=True)  117 us
    psum x2, blocking collectives, squared_norm(): return lax.psum(jnp.sum(values * values, axis=(1, 2)), ('sub', 'grp'))  80.2 us
    psum x1, blocking collectives, shards(): lower = jnp.linalg.cholesky(lax.psum(gram_local, ('sub', 'grp')))  40.1 us
    psum x1, blocking collectives, shards(): projection = lax.psum(projection_part, ('sub', 'grp'))  38.3 us
    psum x1, blocking collectives, shards(): lax.psum(jnp.sum(direction * image, axis=(1, 2)), ('sub', 'grp'))  38.1 us
    ppermute x8, waiting for transfers between devices, shifted(): lax.ppermute(array, axis, [(i, (i + by) % count) for i in range(count)])  29 us
  transfers between devices with their start and end apart: 9, of which 9 were waited for; matrix products, arithmetic and copies ran while one was open for 2% of the time, Pallas kernels for 0%

commit v1 on v0

--- a/solution.py
+++ b/solution.py
@@ -85,7 +85,7 @@
         middle = jnp.zeros((case_count, sub_count, unknowns - 2 * NI), jnp.float32)
         image_field = apply_green(jnp.concatenate([-left_parts, middle, direction], axis=2))
         image = interface_jump(image_field)
-        curvature = lax.psum(jnp.sum(direction * image, axis=(1, 2)), ("sub", "grp"))
+        curvature = lax.psum(lax.psum(jnp.sum(direction * image, axis=(1, 2)), "grp"), "sub")
         alpha = (norm_now / curvature)[:, None, None]
         carried = carried - alpha * image_field
         residual = residual - alpha * image

time: 397 us -> 411 us (1.035)
  blocking collectives: 314 us -> 331 us
    psum x1 -> x4, blocking collectives: 38.1 us -> 57.3 us  [the longest x2 45.7 us: shards(): lax.psum(lax.psum(jnp.sum(direction * image, axis=(1, 2)), 'grp'), 'sub')]
where the time goes in v1:
time: 411 us; the launch traced here: 410 us
  blocking collectives  331 us (81%)
  waiting for transfers between devices  33.5 us (8%)
  matrix products  17.6 us (4%)
  local copies, waits for them, and re-layouts  13.2 us (3%)
  other arithmetic  6.97 us (2%)
  starting transfers between devices  6.59 us (2%)
    all_gather x3, blocking collectives, apply_green(): lax.all_gather(flat_terms, ('sub', 'grp'), axis=1, tiled=True)  118 us
    psum x2, blocking collectives, squared_norm(): return lax.psum(jnp.sum(values * values, axis=(1, 2)), ('sub', 'grp'))  78 us
    psum x2, blocking collectives, shards(): lax.psum(lax.psum(jnp.sum(direction * image, axis=(1, 2)), 'grp'), 'sub')  45.7 us
    psum x1, blocking collectives, shards(): lower = jnp.linalg.cholesky(lax.psum(gram_local, ('sub', 'grp')))  40.1 us
    psum x1, blocking collectives, shards(): projection = lax.psum(projection_part, ('sub', 'grp'))  38.3 us
    ppermute x8, waiting for transfers between devices, shifted(): lax.ppermute(array, axis, [(i, (i + by) % count) for i in range(count)])  29 us
    psum x2, blocking collectives, shards(): lax.psum(jnp.sum(direction * image, axis=(1, 2)), 'grp')  11.5 us
  transfers between devices with their start and end apart: 9, of which 9 were waited for; matrix products, arithmetic and copies ran while one was open for 2% of the time, Pallas kernels for 0%

profile of v1, /device:TPU:0, one launch (start us, length us, event | category | flops | bytes accessed | tf_op | source)
XLA Modules:
  0.0 410.0 jit_solution(17074023163622557388)
XLA Ops:
  0.7 1.5 copy.65
  2.2 1.1 slice.101
  3.4 0.3 convolution_bitcast_fusion.3
  3.8 43.6 %all_gather.9 = f32[8,4096]{1,0:T(8,128)S(1)} all-gather(f32[8,128]{1,0:T(8,128)S(1)} %reshape.67), channel_id=1, replica_groups=mesh['sub'=8,'grp'=4] {'sub','grp'}, dimensions={1}, use_global_device_ids=true | all-gather | bytes 135168 | tf_op jit(solution)/shard_map/all_gather | solution.py:54
  47.4 1.3 pad_maximum_fusion.1
  48.7 0.2 pad_maximum_fusion
  48.9 1.3 copy-done.1
  50.2 1.1 fusion.49
  51.4 0.4 collective-permute-start
  51.8 1.8 fusion.10
  53.7 4.4 %collective-permute-done = f32[8,32]{1,0:T(8,128)S(1)} collective-permute-done((f32[8,32]{1,0:T(8,128)S(1)}, f32[8,32]{1,0:T(8,128)S(1)}, u32[]{:S(2)}, u32[]{:S(2)}) %collective-permute-start) | collective-permute-done | bytes 1056 | tf_op jit(solution)/shard_map/ppermute | solution.py:18
  58.1 0.3 fusion.2
  58.4 0.7 collective-permute-start.1
  59.0 1.3 collective-permute-done.1
  60.4 6.6 %collective-permute-done.2 = f32[8,1,128]{2,0,1:T(8,128)S(1)} collective-permute-done((f32[8,1,128]{2,0,1:T(8,128)S(1)}, f32[8,1,128]{2,0,1:T(8,128)S(1)}, u32[]{:S(2)}, u32[]{:S(2)}) %collective-permute-start.2) | collective-permute-done | bytes 4128 | tf_op jit(solution)/shard_map/ppermute | solution.py:18
  67.0 0.3 convolution_bitcast_fusion.2
  67.4 36.7 %all_gather.10 = f32[8,4096]{1,0:T(8,128)S(1)} all-gather(f32[8,128]{1,0:T(8,128)S(1)} %reshape.73), channel_id=1, replica_groups=mesh['sub'=8,'grp'=4] {'sub','grp'}, dimensions={1}, use_global_device_ids=true | all-gather | bytes 135168 | tf_op jit(solution)/shard_map/all_gather | solution.py:54
  104.1 2.7 fusion.50
  106.9 0.4 collective-permute-start.3
  107.2 1.8 fusion.5
  109.1 4.4 %collective-permute-done.3 = f32[8,32]{1,0:T(8,128)S(1)} collective-permute-done((f32[8,32]{1,0:T(8,128)S(1)}, f32[8,32]{1,0:T(8,128)S(1)}, u32[]{:S(2)}, u32[]{:S(2)}) %collective-permute-start.3) | collective-permute-done | bytes 1056 | tf_op jit(solution)/shard_map/ppermute | solution.py:18
  113.5 0.3 fusion.1
  113.8 0.7 collective-permute-start.4
  114.5 1.3 collective-permute-done.4
  116.0 5.8 %psum.57 = f32[8]{0:T(128)S(1)} all-reduce(f32[8]{0:T(128)S(1)} %get-tuple-element.20), channel_id=1, replica_groups=mesh['sub'=8,'grp'=4] {'grp'}, use_global_device_ids=true, to_apply=%region_3.4 | all-reduce | flops 8 | bytes 64 | tf_op jit(solution)/shard_map/psum | solution.py:88
  121.7 22.9 %psum.58 = f32[8]{0:T(128)S(1)} all-reduce(f32[8]{0:T(128)S(1)} %psum.57), channel_id=1, replica_groups=mesh['sub'=8,'grp'=4] {'sub'}, use_global_device_ids=true, to_apply=%region_4.5 | all-reduce | flops 8 | bytes 64 | tf_op jit(solution)/shard_map/psum | solution.py:88
  144.6 36.8 %psum.56 = f32[8]{0:T(128)S(1)} all-reduce(f32[8]{0:T(128)S(1)} %get-tuple-element.21), channel_id=1, replica_groups=mesh['sub'=8,'grp'=4] {'sub','grp'}, use_global_device_ids=true, to_apply=%region_1.2 | all-reduce | flops 8 | bytes 64 | tf_op jit(solution)/shard_map/psum | solution.py:72
  181.4 0.2 multiply_reduce_fusion
  181.6 41.2 %psum.59 = f32[8]{0:T(128)S(1)} all-reduce(f32[8]{0:T(128)S(1)} %multiply_reduce_fusion), channel_id=1, replica_groups=mesh['sub'=8,'grp'=4] {'sub','grp'}, use_global_device_ids=true, to_apply=%region_6.7 | all-reduce | flops 8 | bytes 64 | tf_op jit(solution)/shard_map/psum | solution.py:72
  222.9 6.6 %collective-permute-done.5 = f32[8,1,128]{2,0,1:T(8,128)S(1)} collective-permute-done((f32[8,1,128]{2,0,1:T(8,128)S(1)}, f32[8,1,128]{2,0,1:T(8,128)S(1)}, u32[]{:S(2)}, u32[]{:S(2)}) %collective-permute-start.5) | collective-permute-done | bytes 4128 | tf_op jit(solution)/shard_map/ppermute | solution.py:18
  229.5 0.3 convolution_bitcast_fusion.1
  229.9 37.4 %all_gather.11 = f32[8,4096]{1,0:T(8,128)S(1)} all-gather(f32[8,128]{1,0:T(8,128)S(1)} %reshape.76), channel_id=1, replica_groups=mesh['sub'=8,'grp'=4] {'sub','grp'}, dimensions={1}, use_global_device_ids=true | all-gather | bytes 135168 | tf_op jit(solution)/shard_map/all_gather | solution.py:54
  267.3 2.7 fusion.51
  270.1 0.5 collective-permute-start.6
  270.6 2.5 fusion.6
  273.1 3.7 collective-permute-done.6
  276.9 1.0 fusion
  277.9 1.4 collective-permute-start.7
  279.3 0.7 scatter_custom_fusion
  280.0 0.6 collective-permute-done.7
  280.8 5.8 %psum.60 = f32[8]{0:T(128)S(1)} all-reduce(f32[8]{0:T(128)S(1)} %fusion.17), channel_id=1, replica_groups=mesh['sub'=8,'grp'=4] {'grp'}, use_global_device_ids=true, to_apply=%region_8.9 | all-reduce | flops 8 | bytes 64 | tf_op jit(solution)/shard_map/psum | solution.py:88
  286.5 22.9 %psum.61 = f32[8]{0:T(128)S(1)} all-reduce(f32[8]{0:T(128)S(1)} %psum.60), channel_id=1, replica_groups=mesh['sub'=8,'grp'=4] {'sub'}, use_global_device_ids=true, to_apply=%region_9.10 | all-reduce | flops 8 | bytes 64 | tf_op jit(solution)/shard_map/psum | solution.py:88
  309.4 1.5 fusion.4
  311.0 0.8 copy.81
  311.9 1.5 gather_fusion
  313.4 0.2 copy.82
  313.7 0.7 reshape.100
  314.4 2.6 all-to-all-start
  317.0 1.4 copy.88
  318.4 1.4 copy.89
  319.8 4.5 %all-to-all-done = f32[32,1,256]{2,1,0:T(1,128)S(1)} async-done(((f32[32,1,256]{2,1,0:T(1,128)}), f32[32,1,256]{2,1,0:T(1,128)S(1)}, u32[]{:S(2)}, u32[]{:S(2)}) %all-to-all-start) | async-done | bytes 32800 | tf_op jit(solution)/shard_map/all_to_all | solution.py:113
  324.3 0.5 broadcast.116
  324.8 0.7 reduce.6
  325.7 0.5 convolution_bitcast_fusion
  326.3 38.3 %psum.62 = f32[256,8]{0,1:T(8,128)S(1)} all-reduce(f32[256,8]{0,1:T(8,128)S(1)} %convolution_bitcast_fusion), channel_id=1, replica_groups=mesh['sub'=8,'grp'=4] {'sub','grp'}, use_global_device_ids=true, to_apply=%region_11.12 | all-reduce | flops 2048 | bytes 16384 | tf_op jit(solution)/shard_map/psum | solution.py:117
  364.5 1.0 convolution_subtract_fusion
  365.5 0.2 fusion.52
  365.6 40.1 %psum.63 = f32[8,8]{0,1:T(8,128)S(1)} all-reduce(f32[8,8]{0,1:T(8,128)S(1)} %fusion.52), channel_id=1, replica_groups=mesh['sub'=8,'grp'=4] {'sub','grp'}, use_global_device_ids=true, to_apply=%region_12.13 | all-reduce | flops 64 | bytes 512 | tf_op jit(solution)/shard_map/psum | solution.py:122
  405.8 0.7 cholesky.18
  406.5 0.6 compare_reduce_fusion
  407.2 0.6 select_bitcast_fusion
  407.8 0.6 custom-call.7
  408.5 0.9 convolution_multiply_fusion
  409.3 0.7 copy.90
  (73 shorter events, 1.9 us)
Async XLA Ops:
  0.6 51.1 %copy-start = (f32[2,512,512]{2,1,0:T(8,128)S(1)}, f32[2,512,512]{2,1,0:T(8,128)}, u32[]{:S(2)}) copy-start(f32[2,512,512]{2,1,0:T(8,128)} %param.10) | copy-start | bytes 6291460
  0.6 2.7 copy-start.6
  0.7 2.7 copy-start.7
  0.7 2.6 copy-start.5
  0.7 2.7 copy-start.2
  2.2 1.1 copy-start.9
  2.2 1.1 copy-start.10
  48.9 1.4 copy-start.1
  51.4 6.7 %collective-permute-start = (f32[8,32]{1,0:T(8,128)S(1)}, f32[8,32]{1,0:T(8,128)S(1)}, u32[]{:S(2)}, u32[]{:S(2)}) collective-permute-start(f32[8,32]{1,0:T(8,128)S(1)} %slice.79), channel_id=1, source_target_pairs={{0,1},{1,2},{2,3},{3,4},{4,5},{5,6},{6,7},{7,8},{8,9},{9,10},{10,1... | collective-permute-start | bytes 3080 | tf_op jit(solution)/shard_map/ppermute | solution.py:18
  58.4 2.0 collective-permute-start.1
  60.4 6.6 %collective-permute-start.2 = (f32[8,1,128]{2,0,1:T(8,128)S(1)}, f32[8,1,128]{2,0,1:T(8,128)S(1)}, u32[]{:S(2)}, u32[]{:S(2)}) collective-permute-start(f32[8,1,128]{2,0,1:T(8,128)S(1)} %get-tuple-element.32), channel_id=1, source_target_pairs={{0,1},{1,2},{2,3},{3,4},{4,5},{5,6},{6,7},{7,8},{8,9},{9,10},{10,1... | collective-permute-start | bytes 12296 | tf_op jit(solution)/shard_map/ppermute | solution.py:18
  106.9 6.6 %collective-permute-start.3 = (f32[8,32]{1,0:T(8,128)S(1)}, f32[8,32]{1,0:T(8,128)S(1)}, u32[]{:S(2)}, u32[]{:S(2)}) collective-permute-start(f32[8,32]{1,0:T(8,128)S(1)} %slice.86), channel_id=1, source_target_pairs={{0,1},{1,2},{2,3},{3,4},{4,5},{5,6},{6,7},{7,8},{8,9},{9,10},{10,1... | collective-permute-start | bytes 3080 | tf_op jit(solution)/shard_map/ppermute | solution.py:18
  113.8 2.0 collective-permute-start.4
  222.9 6.6 %collective-permute-start.5 = (f32[8,1,128]{2,0,1:T(8,128)S(1)}, f32[8,1,128]{2,0,1:T(8,128)S(1)}, u32[]{:S(2)}, u32[]{:S(2)}) collective-permute-start(f32[8,1,128]{2,0,1:T(8,128)S(1)} %get-tuple-element.30), channel_id=1, source_target_pairs={{0,1},{1,2},{2,3},{3,4},{4,5},{5,6},{6,7},{7,8},{8,9},{9,10},{10,1... | collective-permute-start | bytes 12296 | tf_op jit(solution)/shard_map/ppermute | solution.py:18
  267.3 12.0 %copy-start.11 = (s32[32]{0:T(128)S(1)}, s32[32]{0:T(128)}, u32[]{:S(2)}) copy-start(s32[32]{0:T(128)} %param.19) | copy-start | bytes 388
  270.1 6.8 %collective-permute-start.6 = (f32[8,32]{1,0:T(8,128)S(1)}, f32[8,32]{1,0:T(8,128)S(1)}, u32[]{:S(2)}, u32[]{:S(2)}) collective-permute-start(f32[8,32]{1,0:T(8,128)S(1)} %slice.93), channel_id=1, source_target_pairs={{0,1},{1,2},{2,3},{3,4},{4,5},{5,6},{6,7},{7,8},{8,9},{9,10},{10,1... | collective-permute-start | bytes 3080 | tf_op jit(solution)/shard_map/ppermute | solution.py:18
  273.1 52.7 %copy-start.3 = (f32[1024,256]{1,0:T(8,128)S(1)}, f32[1024,256]{1,0:T(8,128)}, u32[]{:S(2)}) copy-start(f32[1024,256]{1,0:T(8,128)} %param.18) | copy-start | bytes 3145732
  277.9 2.7 collective-permute-start.7
  310.9 2.5 copy-start.4
  314.4 9.8 %all-to-all-start = ((f32[32,1,256]{2,1,0:T(1,128)}), f32[32,1,256]{2,1,0:T(1,128)S(1)}, u32[]{:S(2)}, u32[]{:S(2)}) async-start(f32[32,1,256]{2,1,0:T(1,128)} %reshape.100), calls=%async_computation | async-start | bytes 65536 | tf_op jit(solution)/shard_map/all_to_all | solution.py:113
  364.5 45.5 %copy-start.8 = (f32[256,8]{0,1:T(8,128)}, f32[256,8]{0,1:T(8,128)S(1)}, u32[]{:S(2)}) copy-start(f32[256,8]{0,1:T(8,128)S(1)} %psum.62) | copy-start | bytes 24580
